TPU v7x, 32 devices: a whole 2x2x4 slice. The times are simulated.
32 devices in a mesh: date: 4 (over y, x), pix: 8 (over z, core).
Axes of the slice: x: 2, y: 2, z: 4, core: 2. Of those that a mesh axis runs over, the one named last changes fastest.
Arguments:
- stack: bfloat16 [64, 7, 64, 1024], P('date', None, None, 'pix'), may hold values from -8 to 8
- quality: int32 [64, 64, 1024], P('date', None, 'pix'), may hold values from 0 to 1073741823
- days: int32 [64], P('date'), may hold values from 8 to 1536, as said below
Outputs:
- coef: float32 [7, 8, 64, 1024], P(None, None, 'pix', 'date')
- score: float32 [7, 64, 1024], P(None, 'pix', 'date')
Inputs may be any that keep to these rules, and one draw needn't show every extreme that they name: `days`: strictly increasing.
All inputs are finite; a program needn't handle non-finite values.
Results may differ from a plain program's by a relative error of at most 0.0003.
Values may be sent and summed in bfloat16 or wider, within the bound.
A program may use at most 256 MiB of HBM per device.

v0:
```python
import functools

import jax
import jax.numpy as jnp
from jax import lax
from jax.experimental import pallas as pl
from jax.experimental.pallas import tpu as pltpu
from jax.sharding import PartitionSpec as P

RIDGE_TERM = 1.0
HARM = 8
LAG = 4
EARLY = 1
LIMIT = 32767.0


def ORDER(dates):
    return range(dates - 1, 0, -1)
MESH = pl.DeviceIdType.MESH
PAIR_LIST = [(first, second) for first in range(HARM) for second in range(first + 1)]
PAIR_AT = {pair: number for number, pair in enumerate(PAIR_LIST)}


def design_lanes(days):
    rows = [jnp.full((1, 128), day, jnp.int32) for day in days]
    moment_t = jnp.concatenate(rows, 0).astype(jnp.float32)
    lane = lax.broadcasted_iota(jnp.int32, moment_t.shape, 1)
    rate = jnp.where(
        lane < 4, 2.0 * jnp.pi, jnp.where(lane < 6, 4.0 * jnp.pi, 6.0 * jnp.pi))
    phase = rate * moment_t / 365.25
    wave = jnp.where(jnp.bitwise_and(lane, 1) == 0, jnp.cos(phase), jnp.sin(phase))
    linear = (moment_t - 512.0) / 512.0
    return jnp.where(lane == 0, 1.0, jnp.where(lane == 1, linear, wave))


def kernel(dims, stack, quality, days, fin, tot_ref,
           des_in, qbuf, code, raw, dall, bdes, wbuf, lbuf, wsum_ref, res, rel,
           ssum, part, part_date, part_mid, part_pix,
           q_sem, des_send, des_recv, raw_send, raw_recv,
           hop_send, rel_recv, fin_send, fin_recv,
           pd_send, pd_recv, pp_send, pp_recv):
    dates, pixes, times, bands, block = dims
    per = pixes // dates
    s = lax.axis_index("date")
    q = lax.axis_index("pix")
    total = dates * times

    def peer_of(k):
        if dates & (dates - 1):
            return lax.rem(s + k, dates)
        return jnp.bitwise_xor(s, k)

    home = q // per

    def target(sd, j):
        return per * lax.rem(sd + per * lax.rem(q, 2) + j, dates) + j

    def owner(qq, p):
        shift = per * lax.rem(qq, 2) + lax.rem(p, per)
        return lax.rem(p // per + 64 * dates - shift, dates)

    barrier = pltpu.get_barrier_semaphore()
    for k in range(1, dates):
        pl.semaphore_signal(barrier, inc=1, device_id=(peer_of(k), q),
                            device_id_type=MESH)
    for k in range(1, pixes):
        pl.semaphore_signal(barrier, inc=1, device_id=(s, lax.rem(q + k, pixes)),
                            device_id_type=MESH)

    q_copy = pltpu.make_async_copy(quality, qbuf, q_sem)
    q_copy.start()

    def own_copy(j, b):
        rows = pl.ds(pl.multiple_of(target(s, j) * block, block), block)
        return pltpu.make_async_copy(
            stack.at[:, b, rows, :], raw.at[j, b, pl.ds(s * times, times)],
            raw_recv.at[j, b, s])

    def own_code(j):
        return pltpu.make_async_copy(
            code.at[target(s, j)], raw.at[j, bands, pl.ds(s * times, times)],
            raw_recv.at[j, bands, s])

    for j in range(per):
        for b in range(bands):
            own_copy(j, b).start()

    pl.semaphore_wait(barrier, dates - 1 + pixes - 1)

    def des_copy(k):
        return pltpu.make_async_remote_copy(
            des_in, dall.at[s], des_send.at[k], des_recv.at[s],
            device_id=(peer_of(k), q), device_id_type=MESH)

    def raw_copy(j, b, k):
        peer = peer_of(k)
        rows = pl.ds(pl.multiple_of(target(peer, j) * block, block), block)
        return pltpu.make_async_remote_copy(
            stack.at[:, b, rows, :], raw.at[j, b, pl.ds(s * times, times)],
            raw_send.at[j, b, k], raw_recv.at[j, b, s],
            device_id=(peer, q), device_id_type=MESH)

    def code_copy(j, k):
        peer = peer_of(k)
        return pltpu.make_async_remote_copy(
            code.at[target(peer, j)], raw.at[j, bands, pl.ds(s * times, times)],
            raw_send.at[j, bands, k], raw_recv.at[j, bands, s],
            device_id=(peer, q), device_id_type=MESH)

    for b in range(EARLY):
        for k in ORDER(dates):
            raw_copy(0, b, k).start()

    des_in[...] = design_lanes([days[r] for r in range(times)])
    q_copy.wait()
    for p in range(pixes):
        bits = qbuf[:, p * block:(p + 1) * block, :]
        cloud = jnp.bitwise_and(jnp.right_shift(bits, 3), 1)
        level = jnp.bitwise_and(jnp.right_shift(bits, 8), 3)
        code[p] = ((1 - cloud) * (1 + level)).astype(jnp.float32).astype(jnp.bfloat16)

    for k in range(1, dates):
        des_copy(k).start()
    for j in range(per):
        own_code(j).start()
        for k in range(1, dates):
            code_copy(j, k).start()
    for j in range(per):
        for b in range(EARLY if j == 0 else 0, bands):
            for k in ORDER(dates):
                raw_copy(j, b, k).start()

    def raw_wait(j, b, sd):
        pltpu.make_async_copy(
            raw.at[j, b, pl.ds(sd * times, times)],
            raw.at[j, b, pl.ds(sd * times, times)],
            raw_recv.at[j, b, sd]).wait()

    dall[s] = des_in[...]
    for k in range(1, dates):
        sd = peer_of(k)
        pltpu.make_async_copy(dall.at[sd], dall.at[sd], des_recv.at[sd]).wait()

    @pl.loop(0, total, unroll=4)
    def _(t):
        row = dall[t // times, pl.ds(lax.rem(t, times), 1), :]
        for i in range(HARM):
            bdes[t, i] = jnp.broadcast_to(row[:, i:i + 1], (block, 128))

    zero = jnp.zeros((block, 128), jnp.float32)
    for b in range(bands + 1):
        ssum[b] = zero

    def gram_step(j):
        for sd in range(dates):
            raw_wait(j, bands, sd)

        def body(t, carry):
            value = raw[j, bands, t].astype(jnp.float32)
            w = jnp.where(value == 0.0, 0.0, 1.0 / jnp.maximum(value, 1.0))
            wbuf[t] = w
            d = [bdes[t, i] for i in range(HARM)]
            wd = [w] + [w * d[i] for i in range(1, HARM)]
            return tuple(
                carry[n] + (wd[first] if second == 0 else wd[first] * d[second])
                for n, (first, second) in enumerate(PAIR_LIST))

        gram = lax.fori_loop(0, total, body, (zero,) * len(PAIR_LIST), unroll=2)
        wsum_ref[...] = gram[0]
        ssum[bands] = ssum[bands] + gram[0]
        lower = {}
        for first in range(HARM):
            for second in range(first + 1):
                value = gram[PAIR_AT[first, second]]
                if first == second:
                    value = value + RIDGE_TERM
                for inner in range(second):
                    value = value - lower[first, inner] * lower[second, inner]
                if first == second:
                    lower[first, first] = 1.0 / jnp.sqrt(value)
                else:
                    lower[first, second] = value * lower[second, second]
                lbuf[PAIR_AT[first, second]] = lower[first, second]

    def hop(j, b, start):
        p = target(s, j)

        def act(dst, sem):
            @pl.when(p != q)
            def _():
                c = pltpu.make_async_remote_copy(
                    res.at[j, b], dst, hop_send.at[j, b], sem,
                    device_id=(s, p), device_id_type=MESH)
                c.start() if start else c.wait_send()

            if start:
                @pl.when(p == q)
                def _():
                    pltpu.make_async_copy(res.at[j, b], dst, sem).start()

        @pl.when(home == s)
        def _():
            act(fin.at[lax.rem(q, per), b], fin_recv.at[lax.rem(q, per), b])

        @pl.when(home != s)
        def _():
            act(rel.at[q, b], rel_recv.at[q, b])

    def band_step(j, b):
        for sd in range(dates):
            raw_wait(j, b, sd)

        def body(t, carry):
            wy = wbuf[t] * raw[j, b, t].astype(jnp.float32)
            return tuple(
                carry[i] + (wy if i == 0 else bdes[t, i] * wy) for i in range(HARM))

        moment = lax.fori_loop(0, total, body, (zero,) * HARM, unroll=8)
        low = lambda first, second: lbuf[PAIR_AT[first, second]]
        forward = []
        for first in range(HARM):
            value = moment[first]
            for inner in range(first):
                value = value - low(first, inner) * forward[inner]
            forward.append(value * low(first, first))
        back = [None] * HARM
        for first in range(HARM - 1, -1, -1):
            value = forward[first]
            for inner in range(HARM - 1, first, -1):
                value = value - low(inner, first) * back[inner]
            back[first] = value * low(first, first)
        peak = jnp.abs(back[0])
        for i in range(1, HARM):
            peak = jnp.maximum(peak, jnp.abs(back[i]))
        level = power(peak)
        inverse = jnp.exp2(-level)
        for i in range(HARM):
            res[j, b, i] = encode(back[i], inverse)

        def residual(t, ssr):
            terms = [back[0]] + [bdes[t, i] * back[i] for i in range(1, HARM)]
            while len(terms) > 1:
                terms = [terms[i] + terms[i + 1] for i in range(0, len(terms), 2)]
            diff = raw[j, b, t].astype(jnp.float32) - terms[0]
            return ssr + wbuf[t] * diff * diff

        ssr = lax.fori_loop(0, total, residual, zero, unroll=8)
        ratio = jnp.sqrt(ssr / (wsum_ref[...] + 1.0))
        ratio_level = power(ratio)
        res[j, b, HARM] = encode(ratio, jnp.exp2(-ratio_level))
        lane = lax.broadcasted_iota(jnp.int32, ratio.shape, 1)
        both = jnp.where(lane == 0, level, ratio_level)
        res[j, b, HARM + 1] = both.astype(jnp.int32).astype(jnp.int16)
        ssum[b] = ssum[b] + ssr
        hop(j, b, True)

    def pass_on(qq, b, start):
        far = qq // per

        @pl.when(jnp.logical_and(owner(qq, q) == s, far != s))
        def _():
            c = pltpu.make_async_remote_copy(
                rel.at[qq, b], fin.at[lax.rem(qq, per), b], fin_send.at[qq, b],
                fin_recv.at[lax.rem(qq, per), b],
                device_id=(far, q), device_id_type=MESH)
            if start:
                pltpu.make_async_copy(rel.at[qq, b], rel.at[qq, b], rel_recv.at[qq, b]).wait()
                c.start()
            else:
                c.wait_send()

    def relay(n):
        b = lax.rem(n, bands)

        @pl.when(n // bands == lax.rem(q, per))
        def _():
            @pl.loop(0, pixes)
            def _(qq):
                pass_on(qq, b, True)

    @pl.loop(0, per * bands)
    def _(n):
        j = n // bands
        b = lax.rem(n, bands)

        @pl.when(b == 0)
        def _():
            gram_step(j)

        band_step(j, b)

        @pl.when(n >= LAG)
        def _():
            relay(n - LAG)

    part[...] = jnp.concatenate(
        [jnp.sum(ssum[b], 0, keepdims=True) for b in range(bands + 1)], 0)

    def date_part(k):
        return pltpu.make_async_remote_copy(
            part, part_date.at[s], pd_send.at[k], pd_recv.at[s],
            device_id=(peer_of(k), q), device_id_type=MESH)

    def pix_part(k):
        return pltpu.make_async_remote_copy(
            part_mid, part_pix.at[q], pp_send.at[k], pp_recv.at[q],
            device_id=(s, lax.rem(q + k, pixes)), device_id_type=MESH)

    for k in range(1, dates):
        date_part(k).start()
    part_date[s] = part[...]
    for n in range(LAG):
        relay(per * bands - LAG + n)
    for k in range(1, dates):
        sd = peer_of(k)
        pltpu.make_async_copy(part_date.at[sd], part_date.at[sd], pd_recv.at[sd]).wait()
    mid = part_date[0]
    for sd in range(1, dates):
        mid = mid + part_date[sd]
    part_mid[...] = mid
    for k in range(1, pixes):
        pix_part(k).start()
    part_pix[q] = mid

    @pl.loop(0, bands)
    def _(b):
        for c in range(per):
            pltpu.make_async_copy(fin.at[c, b], fin.at[c, b], fin_recv.at[c, b]).wait()

    for k in range(1, pixes):
        qq = lax.rem(q + k, pixes)
        pltpu.make_async_copy(part_pix.at[qq], part_pix.at[qq], pp_recv.at[qq]).wait()
    tot = part_pix[0]
    for qq in range(1, pixes):
        tot = tot + part_pix[qq]
    tot_ref[...] = tot

    for k in range(1, dates):
        des_copy(k).wait_send()
        date_part(k).wait_send()
    for k in range(1, pixes):
        pix_part(k).wait_send()

    @pl.loop(0, per)
    def _(j):
        for k in range(1, dates):
            code_copy(j, k).wait_send()

        @pl.loop(0, bands)
        def _(b):
            for k in range(1, dates):
                raw_copy(j, b, k).wait_send()
            hop(j, b, False)

    @pl.loop(0, pixes)
    def _(qq):
        @pl.loop(0, bands)
        def _(b):
            pass_on(qq, b, False)


def power(value):
    peak = jnp.max(jnp.max(value, 0, keepdims=True), 1, keepdims=True)
    level = jnp.ceil(jnp.log2(jnp.maximum(peak, 1e-36)) + 0.01)
    return jnp.broadcast_to(level, value.shape)


def encode(value, inverse):
    root = jnp.sqrt(jnp.minimum(jnp.abs(value) * inverse, 1.0)) * LIMIT + 0.5
    root = jnp.floor(root)
    return jnp.where(value < 0.0, -root, root).astype(jnp.int32).astype(jnp.int16)


def decode(value, scale):
    root = value.astype(jnp.int32).astype(jnp.float32) * (1.0 / LIMIT)
    return root * jnp.abs(root) * scale


def finish(fin, tot_ref, coef, score):
    per, bands = fin.shape[:2]
    tot = jnp.sum(tot_ref[...], 1, keepdims=True)
    for b in range(bands):
        sigma = jnp.sqrt(tot[b:b + 1] / tot[bands:bands + 1])
        scale = jnp.broadcast_to(1.0 / sigma, fin.shape[3:])
        for c in range(per):
            cols = slice(c * 128, (c + 1) * 128)
            both = fin[c, b, HARM + 1].astype(jnp.int32).astype(jnp.float32)
            unit = jnp.broadcast_to(jnp.exp2(both[:, 0:1]), both.shape)
            ratio_unit = jnp.broadcast_to(jnp.exp2(both[:, 1:2]), both.shape)
            for i in range(HARM):
                coef[b, i, :, cols] = decode(fin[c, b, i], unit)
            score[b, :, cols] = decode(fin[c, b, HARM], ratio_unit) * scale


def local(mesh, stack, quality, days):
    dates, pixes = mesh.shape["date"], mesh.shape["pix"]
    times, bands, rows, width = stack.shape
    block = rows // pixes
    per = pixes // dates
    total = dates * times
    dims = (dates, pixes, times, bands, block)
    tile = (block, width)
    vmem, dma = pltpu.VMEM, pltpu.SemaphoreType.DMA
    f32, bf16 = jnp.float32, jnp.bfloat16
    fin, tot = pl.pallas_call(
        functools.partial(kernel, dims),
        out_shape=(
            jax.ShapeDtypeStruct((per, bands, HARM + 2) + tile, jnp.int16),
            jax.ShapeDtypeStruct((bands + 1, width), f32),
        ),
        in_specs=[
            pl.BlockSpec(memory_space=pl.ANY),
            pl.BlockSpec(memory_space=pl.ANY),
            pl.BlockSpec(memory_space=pltpu.SMEM),
        ],
        out_specs=(
            pl.BlockSpec(memory_space=pl.ANY),
            pl.BlockSpec(memory_space=pltpu.VMEM),
        ),
        scratch_shapes=[
            vmem((times, 128), f32),
            vmem((times, rows, width), jnp.int32),
            vmem((pixes, times) + tile, bf16),
            vmem((per, bands + 1, total) + tile, bf16),
            vmem((dates, times, 128), f32),
            vmem((total, HARM) + tile, f32),
            vmem((total,) + tile, f32),
            vmem((len(PAIR_LIST),) + tile, f32),
            vmem(tile, f32),
            vmem((per, bands, HARM + 2) + tile, jnp.int16),
            vmem((pixes, bands, HARM + 2) + tile, jnp.int16),
            vmem((bands + 1,) + tile, f32),
            vmem((bands + 1, width), f32),
            vmem((dates, bands + 1, width), f32),
            vmem((bands + 1, width), f32),
            vmem((pixes, bands + 1, width), f32),
            dma,
            dma((dates,)),
            dma((dates,)),
            dma((per, bands + 1, dates)),
            dma((per, bands + 1, dates)),
            dma((per, bands)),
            dma((pixes, bands)),
            dma((pixes, bands)),
            dma((per, bands)),
            dma((dates,)),
            dma((dates,)),
            dma((pixes,)),
            dma((pixes,)),
        ],
        compiler_params=pltpu.CompilerParams(
            collective_id=0, has_side_effects=True, vmem_limit_bytes=60000000
        ),
    )(stack, quality, days)
    whole = pl.BlockSpec(memory_space=pltpu.VMEM)
    return pl.pallas_call(
        finish,
        out_shape=(
            jax.ShapeDtypeStruct((bands, HARM, block, width * per), f32),
            jax.ShapeDtypeStruct((bands, block, width * per), f32),
        ),
        in_specs=[whole, whole],
        out_specs=(whole, whole),
    )(fin, tot)


def solution(mesh):
    return jax.shard_map(
        functools.partial(local, mesh),
        mesh=mesh,
        in_specs=(P("date", None, None, "pix"), P("date", None, "pix"), P("date")),
        out_specs=(P(None, None, "pix", "date"), P(None, "pix", "date")),
        check_vma=False,
    )
```

profile of v0, /device:TPU:0, one launch (start us, length us, event | category | flops | bytes accessed | tf_op | source)
XLA Modules:
  0.0 45.8 jit_solution(16874051362779326340)
XLA Ops:
  0.6 43.3 %shard_map.50 = (s16[2,7,10,8,128]{4,3,2,1,0:T(8,128)(2,1)}, f32[8,128]{1,0:T(8,128)}) custom-call(bf16[16,7,64,128]{3,2,1,0:T(8,128)(2,1)} %stack.1, s32[16,64,128]{2,1,0:T(8,128)} %quality.1, s32[16]{0:T(128)} %days.1), custom_call_target="tpu_custom_call" | custom-call | tf_op jit(solution)/shard_map/pallas_call | solution.py:405
  43.9 1.9 %shard_map.51 = (f32[7,8,8,256]{3,2,1,0:T(8,128)}, f32[7,8,256]{2,1,0:T(8,128)}) custom-call(s16[2,7,10,8,128]{4,3,2,1,0:T(8,128)(2,1)} %get-tuple-element.4.fin, f32[8,128]{1,0:T(8,128)} %get-tuple-element.5.tot_ref), custom_call_target="tpu_custom_call" | custom-call | tf_op jit(solution)/shard_map/pallas_call | solution.py:456
where the time goes:
time: 46 us; the launch traced here: 45.8 us
  Pallas kernels  45.2 us (98%)
  between operations  0.64 us (1%)
    pallas_call x1, Pallas kernels, local(): pl.pallas_call(functools.partial(kernel, dims), out_shape=(jax.ShapeDtype...  43.3 us
    pallas_call x1, Pallas kernels, local(): pl.pallas_call(finish, out_shape=(jax.ShapeDtypeStruct((bands, HARM, bloc...  1.89 us

commit v1 on v0

v1 whole, which is shorter than its diff:
```python
import functools

import jax
import jax.numpy as jnp
from jax import lax
from jax.experimental import pallas as pl
from jax.experimental.pallas import tpu as pltpu
from jax.sharding import PartitionSpec as P

RIDGE_TERM = 1.0
HARM = 8
PAIR = 2
LAG = 2
LIMIT = 32767.0
LEVELS = 0x346C

MESH = pl.DeviceIdType.MESH
PAIR_LIST = [(first, second) for first in range(HARM) for second in range(first + 1)]
PAIR_AT = {pair: number for number, pair in enumerate(PAIR_LIST)}


def design_lanes(days):
    rows = [jnp.full((1, 128), day, jnp.int32) for day in days]
    moment_t = jnp.concatenate(rows, 0).astype(jnp.float32)
    lane = lax.broadcasted_iota(jnp.int32, moment_t.shape, 1)
    rate = jnp.where(
        lane < 4, 2.0 * jnp.pi, jnp.where(lane < 6, 4.0 * jnp.pi, 6.0 * jnp.pi))
    phase = rate * moment_t / 365.25
    wave = jnp.where(jnp.bitwise_and(lane, 1) == 0, jnp.cos(phase), jnp.sin(phase))
    linear = (moment_t - 512.0) / 512.0
    return jnp.where(lane == 0, 1.0, jnp.where(lane == 1, linear, wave))


def kernel(dims, stack, quality, days, fin, tot_ref,
           des_in, qbuf, code, raw, dall, bdes, wbuf, lbuf, wsum_ref, res, rel,
           ssum, part, part_date, part_mid, part_pix,
           q_sem, des_send, des_recv, raw_send, raw_recv,
           hop_send, rel_recv, fin_send, fin_recv,
           pd_send, pd_recv, pp_send, pp_recv):
    dates, pixes, times, bands, block = dims
    per = pixes // dates
    units = per // PAIR
    tall = PAIR * block
    s = lax.axis_index("date")
    q = lax.axis_index("pix")
    total = dates * times
    place = lax.rem(q, per)
    home = q // per

    def peer_of(k):
        if dates & (dates - 1):
            return lax.rem(s + k, dates)
        return jnp.bitwise_xor(s, k)

    def group(sd):
        flip = lax.rem(q, 2)
        if dates & (dates - 1):
            return lax.rem(home + flip * (dates // 2) + 2 * dates - sd, dates)
        return jnp.bitwise_xor(jnp.bitwise_xor(home, sd), flip * (dates - 1))

    def far_of(r):
        flip = lax.rem(r, 2)
        if dates & (dates - 1):
            return lax.rem(home + s + dates - flip * (dates // 2), dates)
        return jnp.bitwise_xor(jnp.bitwise_xor(home, s), flip * (dates - 1))

    mine = group(s)

    barrier = pltpu.get_barrier_semaphore()
    for k in range(1, dates):
        pl.semaphore_signal(barrier, inc=1, device_id=(peer_of(k), q),
                            device_id_type=MESH)
    for k in range(1, pixes):
        pl.semaphore_signal(barrier, inc=1, device_id=(s, lax.rem(q + k, pixes)),
                            device_id_type=MESH)

    q_copy = pltpu.make_async_copy(quality, qbuf, q_sem)
    q_copy.start()

    def rows_of(g, u):
        first = (g * units + u) * tall
        return pl.ds(pl.multiple_of(first, tall), tall)

    def mine_at(sd):
        return pl.ds(pl.multiple_of(sd * times, times), times)

    for u in range(units):
        for b in range(bands):
            pltpu.make_async_copy(
                stack.at[:, b, rows_of(mine, u), :], raw.at[u, b, mine_at(s)],
                raw_recv.at[u, b, s]).start()

    des_in[...] = design_lanes([days[r] for r in range(times)])
    q_copy.wait()
    for g in range(dates):
        for u in range(units):
            first = (g * units + u) * tall
            bits = qbuf[:, first:first + tall, :]
            digit = jnp.bitwise_and(jnp.right_shift(bits, 6), 12)
            value = jnp.bitwise_and(jnp.right_shift(jnp.full_like(bits, LEVELS), digit), 15)
            value = jnp.where(jnp.bitwise_and(bits, 8) == 0, value, 0)
            code[g, u] = value.astype(jnp.float32).astype(jnp.bfloat16)

    pl.semaphore_wait(barrier, dates - 1 + pixes - 1)

    def des_copy(k):
        return pltpu.make_async_remote_copy(
            des_in, dall.at[s], des_send.at[k], des_recv.at[s],
            device_id=(peer_of(k), q), device_id_type=MESH)

    def raw_copy(u, b, k):
        peer = peer_of(k)
        return pltpu.make_async_remote_copy(
            stack.at[:, b, rows_of(group(peer), u), :], raw.at[u, b, mine_at(s)],
            raw_send.at[u, b, k], raw_recv.at[u, b, s],
            device_id=(peer, q), device_id_type=MESH)

    def code_copy(u, k):
        peer = peer_of(k)
        return pltpu.make_async_remote_copy(
            code.at[group(peer), u], raw.at[u, bands, mine_at(s)],
            raw_send.at[u, bands, k], raw_recv.at[u, bands, s],
            device_id=(peer, q), device_id_type=MESH)

    order = range(dates - 1, 0, -1)
    for k in order:
        des_copy(k).start()
    for u in range(units):
        for k in order:
            code_copy(u, k).start()
        for b in range(bands):
            for k in order:
                raw_copy(u, b, k).start()
    for u in range(units):
        pltpu.make_async_copy(
            code.at[mine, u], raw.at[u, bands, mine_at(s)],
            raw_recv.at[u, bands, s]).start()

    def raw_wait(u, b, sd):
        there = raw.at[u, b, mine_at(sd)]
        pltpu.make_async_copy(there, there, raw_recv.at[u, b, sd]).wait()

    dall[s] = des_in[...]

    zero = jnp.zeros((PAIR, block, 128), jnp.float32)
    zero_one = jnp.zeros((block, 128), jnp.float32)
    for b in range(bands + 1):
        ssum[b] = zero_one

    def spread(k):
        sd = peer_of(k)
        if k:
            pltpu.make_async_copy(dall.at[sd], dall.at[sd], des_recv.at[sd]).wait()

        @pl.loop(0, times, unroll=4)
        def _(r):
            row = dall[sd, pl.ds(r, 1), :]
            for i in range(HARM):
                bdes[sd * times + r, i] = jnp.broadcast_to(row[:, i:i + 1], (block, 128))

    for k in range(dates):
        spread(k)

    def pair_of(value):
        return value.astype(jnp.float32).reshape(PAIR, block, 128)

    def by_source(wait, body, carry, unroll):
        def source(k, carry):
            sd = peer_of(k)
            wait(sd)
            return lax.fori_loop(
                0, times, lambda r, c: body(sd * times + r, c), carry, unroll=unroll)

        return lax.fori_loop(0, dates, source, carry)

    def gram_step(u):
        def body(jj):
            def step(t, carry):
                if jj == 0:
                    both = pair_of(raw[u, bands, t]) * (1.0 / 12.0)
                    wbuf[t] = both
                    w = both[0]
                else:
                    w = wbuf[t, jj]
                d = [bdes[t, i] for i in range(HARM)]
                wd = [w] + [w * d[i] for i in range(1, HARM)]
                return tuple(
                    carry[n] + (wd[first] if second == 0 else wd[first] * d[second])
                    for n, (first, second) in enumerate(PAIR_LIST))
            return step

        start = (zero_one,) * len(PAIR_LIST)
        gram = by_source(lambda sd: raw_wait(u, bands, sd), body(0), start, 2)
        for n in range(len(PAIR_LIST)):
            lbuf[n, 0] = gram[n]
        for jj in range(1, PAIR):
            gram = lax.fori_loop(0, total, body(jj), start, unroll=2)
            for n in range(len(PAIR_LIST)):
                lbuf[n, jj] = gram[n]
        gram = [lbuf[n] for n in range(len(PAIR_LIST))]
        wsum_ref[...] = 1.0 / (gram[0] + 1.0)
        ssum[bands] = ssum[bands] + jnp.sum(gram[0], 0)
        lower = {}
        for first in range(HARM):
            for second in range(first + 1):
                value = gram[PAIR_AT[first, second]]
                if first == second:
                    value = value + RIDGE_TERM
                for inner in range(second):
                    value = value - lower[first, inner] * lower[second, inner]
                if first == second:
                    lower[first, first] = lax.rsqrt(value)
                else:
                    lower[first, second] = value * lower[second, second]
                lbuf[PAIR_AT[first, second]] = lower[first, second]

    def hop(u, b, start):
        for jj in range(PAIR):
            p = mine * per + PAIR * u + jj

            def act(dst, sem):
                @pl.when(p != q)
                def _():
                    c = pltpu.make_async_remote_copy(
                        res.at[u, b, jj], dst, hop_send.at[u, b, jj], sem,
                        device_id=(s, p), device_id_type=MESH)
                    c.start() if start else c.wait_send()

                if start:
                    @pl.when(p == q)
                    def _():
                        pltpu.make_async_copy(res.at[u, b, jj], dst, sem).start()

            @pl.when(home == s)
            def _():
                act(fin.at[place, b], fin_recv.at[place, b])

            @pl.when(home != s)
            def _():
                act(rel.at[place, b], rel_recv.at[place, b])

    def band_step(u, b):
        def body(t, carry):
            wy = wbuf[t] * pair_of(raw[u, b, t])
            return tuple(
                carry[i] + (wy if i == 0 else bdes[t, i] * wy) for i in range(HARM))

        moment = by_source(lambda sd: raw_wait(u, b, sd), body, (zero,) * HARM, 8)
        low = lambda first, second: lbuf[PAIR_AT[first, second]]
        forward = []
        for first in range(HARM):
            value = moment[first]
            for inner in range(first):
                value = value - low(first, inner) * forward[inner]
            forward.append(value * low(first, first))
        back = [None] * HARM
        for first in range(HARM - 1, -1, -1):
            value = forward[first]
            for inner in range(HARM - 1, first, -1):
                value = value - low(inner, first) * back[inner]
            back[first] = value * low(first, first)

        def residual(t, ssr):
            terms = [back[0]] + [bdes[t, i] * back[i] for i in range(1, HARM)]
            while len(terms) > 1:
                terms = [terms[i] + terms[i + 1] for i in range(0, len(terms), 2)]
            diff = pair_of(raw[u, b, t]) - terms[0]
            return ssr + wbuf[t] * diff * diff

        ssr = lax.fori_loop(0, total, residual, zero, unroll=8)
        ratio = jnp.sqrt(ssr * wsum_ref[...])
        peak = ratio
        for i in range(HARM):
            peak = jnp.maximum(peak, jnp.abs(back[i]))
        level = jnp.ceil(jnp.log2(jnp.maximum(peak, 1e-36)) + 0.01)
        inverse = jnp.exp2(-level)
        scale = inverse * LIMIT
        for i in range(HARM):
            put(res, u, b, i, jnp.floor(jnp.clip(back[i] * scale, -LIMIT, LIMIT) + 0.5))
        root = jnp.sqrt(jnp.sqrt(jnp.minimum(ratio * inverse, 1.0)))
        put(res, u, b, HARM, jnp.floor(root * LIMIT + 0.5))
        put(res, u, b, HARM + 1, level)
        ssum[b] = ssum[b] + jnp.sum(ssr, 0)
        hop(u, b, True)

    def pass_on(r, b, start):
        far = far_of(r)

        @pl.when(far != s)
        def _():
            c = pltpu.make_async_remote_copy(
                rel.at[r, b], fin.at[r, b], fin_send.at[r, b], fin_recv.at[r, b],
                device_id=(far, q), device_id_type=MESH)
            if start:
                pltpu.make_async_copy(rel.at[r, b], rel.at[r, b], rel_recv.at[r, b]).wait()
                c.start()
            else:
                c.wait_send()

    def relay(n):
        b = lax.rem(n, bands)

        @pl.when(n // bands == place // PAIR)
        def _():
            for r in range(per):
                pass_on(r, b, True)

    @pl.loop(0, units * bands)
    def _(n):
        u = n // bands
        b = lax.rem(n, bands)

        @pl.when(b == 0)
        def _():
            gram_step(u)

        band_step(u, b)

        @pl.when(n >= LAG)
        def _():
            relay(n - LAG)

    part[...] = jnp.concatenate(
        [jnp.sum(ssum[b], 0, keepdims=True) for b in range(bands + 1)], 0)

    def date_part(k):
        return pltpu.make_async_remote_copy(
            part, part_date.at[s], pd_send.at[k], pd_recv.at[s],
            device_id=(peer_of(k), q), device_id_type=MESH)

    def pix_part(k):
        return pltpu.make_async_remote_copy(
            part_mid, part_pix.at[q], pp_send.at[k], pp_recv.at[q],
            device_id=(s, lax.rem(q + k, pixes)), device_id_type=MESH)

    for k in range(1, dates):
        date_part(k).start()
    part_date[s] = part[...]
    for n in range(LAG):
        relay(units * bands - LAG + n)
    for k in range(1, dates):
        sd = peer_of(k)
        pltpu.make_async_copy(part_date.at[sd], part_date.at[sd], pd_recv.at[sd]).wait()
    mid = part_date[0]
    for sd in range(1, dates):
        mid = mid + part_date[sd]
    part_mid[...] = mid
    for k in range(1, pixes):
        pix_part(k).start()
    part_pix[q] = mid

    @pl.loop(0, bands)
    def _(b):
        for r in range(per):
            pltpu.make_async_copy(fin.at[r, b], fin.at[r, b], fin_recv.at[r, b]).wait()

    for k in range(1, pixes):
        qq = lax.rem(q + k, pixes)
        pltpu.make_async_copy(part_pix.at[qq], part_pix.at[qq], pp_recv.at[qq]).wait()
    tot = part_pix[0]
    for qq in range(1, pixes):
        tot = tot + part_pix[qq]
    tot_ref[...] = tot

    for k in range(1, dates):
        des_copy(k).wait_send()
        date_part(k).wait_send()
    for k in range(1, pixes):
        pix_part(k).wait_send()

    @pl.loop(0, units)
    def _(u):
        for k in range(1, dates):
            code_copy(u, k).wait_send()

        @pl.loop(0, bands)
        def _(b):
            for k in range(1, dates):
                raw_copy(u, b, k).wait_send()
            hop(u, b, False)

    @pl.loop(0, bands)
    def _(b):
        for r in range(per):
            pass_on(r, b, False)


def put(res, u, b, i, value):
    whole = value.astype(jnp.int32)
    for jj in range(PAIR):
        res[u, b, jj, i] = whole[jj].astype(jnp.int16)


def finish(fin, tot_ref, coef, score):
    per, bands = fin.shape[:2]
    tot = jnp.sum(tot_ref[...], 1, keepdims=True)
    for b in range(bands):
        sigma = jnp.sqrt(tot[b:b + 1] / tot[bands:bands + 1])
        scale = jnp.broadcast_to(1.0 / sigma, fin.shape[3:])
        for r in range(per):
            cols = slice(r * 128, (r + 1) * 128)
            number = lambda i: fin[r, b, i].astype(jnp.int32).astype(jnp.float32)
            unit = jnp.exp2(number(HARM + 1))
            step = unit * (1.0 / LIMIT)
            for i in range(HARM):
                coef[b, i, :, cols] = number(i) * step
            root = number(HARM) * (1.0 / LIMIT)
            root = root * root
            score[b, :, cols] = root * root * (unit * scale)


def local(mesh, stack, quality, days):
    dates, pixes = mesh.shape["date"], mesh.shape["pix"]
    times, bands, rows, width = stack.shape
    block = rows // pixes
    per = pixes // dates
    units = per // PAIR
    total = dates * times
    dims = (dates, pixes, times, bands, block)
    tile = (block, width)
    both = (PAIR,) + tile
    tall = (PAIR * block, width)
    vmem, dma = pltpu.VMEM, pltpu.SemaphoreType.DMA
    f32, bf16 = jnp.float32, jnp.bfloat16
    fin, tot = pl.pallas_call(
        functools.partial(kernel, dims),
        out_shape=(
            jax.ShapeDtypeStruct((per, bands, HARM + 2) + tile, jnp.int16),
            jax.ShapeDtypeStruct((bands + 1, width), f32),
        ),
        in_specs=[
            pl.BlockSpec(memory_space=pl.ANY),
            pl.BlockSpec(memory_space=pl.ANY),
            pl.BlockSpec(memory_space=pltpu.SMEM),
        ],
        out_specs=(
            pl.BlockSpec(memory_space=pl.ANY),
            pl.BlockSpec(memory_space=pltpu.VMEM),
        ),
        scratch_shapes=[
            vmem((times, 128), f32),
            vmem((times, rows, width), jnp.int32),
            vmem((dates, units, times) + tall, bf16),
            vmem((units, bands + 1, total) + tall, bf16),
            vmem((dates, times, 128), f32),
            vmem((total, HARM) + tile, f32),
            vmem((total,) + both, f32),
            vmem((len(PAIR_LIST),) + both, f32),
            vmem(both, f32),
            vmem((units, bands, PAIR, HARM + 2) + tile, jnp.int16),
            vmem((per, bands, HARM + 2) + tile, jnp.int16),
            vmem((bands + 1,) + tile, f32),
            vmem((bands + 1, width), f32),
            vmem((dates, bands + 1, width), f32),
            vmem((bands + 1, width), f32),
            vmem((pixes, bands + 1, width), f32),
            dma,
            dma((dates,)),
            dma((dates,)),
            dma((units, bands + 1, dates)),
            dma((units, bands + 1, dates)),
            dma((units, bands, PAIR)),
            dma((per, bands)),
            dma((per, bands)),
            dma((per, bands)),
            dma((dates,)),
            dma((dates,)),
            dma((pixes,)),
            dma((pixes,)),
        ],
        compiler_params=pltpu.CompilerParams(
            collective_id=0, has_side_effects=True, vmem_limit_bytes=60000000
        ),
    )(stack, quality, days)
    whole = pl.BlockSpec(memory_space=pltpu.VMEM)
    return pl.pallas_call(
        finish,
        out_shape=(
            jax.ShapeDtypeStruct((bands, HARM, block, width * per), f32),
            jax.ShapeDtypeStruct((bands, block, width * per), f32),
        ),
        in_specs=[whole, whole],
        out_specs=(whole, whole),
    )(fin, tot)


def solution(mesh):
    return jax.shard_map(
        functools.partial(local, mesh),
        mesh=mesh,
        in_specs=(P("date", None, None, "pix"), P("date", None, "pix"), P("date")),
        out_specs=(P(None, None, "pix", "date"), P(None, "pix", "date")),
        check_vma=False,
    )
```

time: 46 us -> 43.7 us (0.950)
  Pallas kernels: 45.2 us -> 42.9 us
    pallas_call x1, Pallas kernels: 43.3 us -> 41.1 us  [local(): pl.pallas_call(functools.partial(kernel, dims), out_shape=(jax.ShapeDtype...]
where the time goes in v1:
time: 43.7 us; the launch traced here: 43.6 us
  Pallas kernels  42.9 us (98%)
  between operations  0.64 us (1%)
    pallas_call x1, Pallas kernels, local(): pl.pallas_call(functools.partial(kernel, dims), out_shape=(jax.ShapeDtype...  41.1 us
    pallas_call x1, Pallas kernels, local(): pl.pallas_call(finish, out_shape=(jax.ShapeDtypeStruct((bands, HARM, bloc...  1.87 us

profile of v1, /device:TPU:0, one launch (start us, length us, event | category | flops | bytes accessed | tf_op | source)
XLA Modules:
  0.0 43.6 jit_solution(10593367179673524147)
XLA Ops:
  0.6 41.1 %shard_map.50 = (s16[2,7,10,8,128]{4,3,2,1,0:T(8,128)(2,1)}, f32[8,128]{1,0:T(8,128)}) custom-call(bf16[16,7,64,128]{3,2,1,0:T(8,128)(2,1)} %stack.1, s32[16,64,128]{2,1,0:T(8,128)} %quality.1, s32[16]{0:T(128)} %days.1), custom_call_target="tpu_custom_call" | custom-call | tf_op jit(solution)/shard_map/pallas_call | solution.py:425
  41.7 1.9 %shard_map.51 = (f32[7,8,8,256]{3,2,1,0:T(8,128)}, f32[7,8,256]{2,1,0:T(8,128)}) custom-call(s16[2,7,10,8,128]{4,3,2,1,0:T(8,128)(2,1)} %get-tuple-element.4.fin, f32[8,128]{1,0:T(8,128)} %get-tuple-element.5.tot_ref), custom_call_target="tpu_custom_call" | custom-call | tf_op jit(solution)/shard_map/pallas_call | solution.py:476

commit v2 on v1

--- a/solution.py
+++ b/solution.py
@@ -10,7 +10,8 @@
 RIDGE_TERM = 1.0
 HARM = 8
 PAIR = 2
-LAG = 2
+LAG = 4
+DIRECT = 1
 LIMIT = 32767.0
 LEVELS = 0x346C
 
@@ -33,10 +34,10 @@
 
 def kernel(dims, stack, quality, days, fin, tot_ref,
            des_in, qbuf, code, raw, dall, bdes, wbuf, lbuf, wsum_ref, res, rel,
-           ssum, part, part_date, part_mid, part_pix,
+           ssum, part, part_all,
            q_sem, des_send, des_recv, raw_send, raw_recv,
            hop_send, rel_recv, fin_send, fin_recv,
-           pd_send, pd_recv, pp_send, pp_recv):
+           part_send, part_recv):
     dates, pixes, times, bands, block = dims
     per = pixes // dates
     units = per // PAIR
@@ -67,11 +68,9 @@
     mine = group(s)
 
     barrier = pltpu.get_barrier_semaphore()
-    for k in range(1, dates):
-        pl.semaphore_signal(barrier, inc=1, device_id=(peer_of(k), q),
-                            device_id_type=MESH)
-    for k in range(1, pixes):
-        pl.semaphore_signal(barrier, inc=1, device_id=(s, lax.rem(q + k, pixes)),
+    others = [(k, kk) for k in range(dates) for kk in range(pixes) if k or kk]
+    for k, kk in others:
+        pl.semaphore_signal(barrier, inc=1, device_id=(peer_of(k), lax.rem(q + kk, pixes)),
                             device_id_type=MESH)
 
     q_copy = pltpu.make_async_copy(quality, qbuf, q_sem)
@@ -101,7 +100,7 @@
             value = jnp.where(jnp.bitwise_and(bits, 8) == 0, value, 0)
             code[g, u] = value.astype(jnp.float32).astype(jnp.bfloat16)
 
-    pl.semaphore_wait(barrier, dates - 1 + pixes - 1)
+    pl.semaphore_wait(barrier, len(others))
 
     def des_copy(k):
         return pltpu.make_async_remote_copy(
@@ -235,9 +234,18 @@
             def _():
                 act(fin.at[place, b], fin_recv.at[place, b])
 
-            @pl.when(home != s)
+            late = u * bands + b >= units * bands - DIRECT
+
+            @pl.when(jnp.logical_and(home != s, jnp.logical_not(late)))
             def _():
                 act(rel.at[place, b], rel_recv.at[place, b])
+
+            @pl.when(jnp.logical_and(home != s, late))
+            def _():
+                c = pltpu.make_async_remote_copy(
+                    res.at[u, b, jj], fin.at[place, b], hop_send.at[u, b, jj],
+                    fin_recv.at[place, b], device_id=(home, p), device_id_type=MESH)
+                c.start() if start else c.wait_send()
 
     def band_step(u, b):
         def body(t, carry):
@@ -320,53 +328,42 @@
         def _():
             relay(n - LAG)
 
-    part[...] = jnp.concatenate(
+    sums = jnp.concatenate(
         [jnp.sum(ssum[b], 0, keepdims=True) for b in range(bands + 1)], 0)
-
-    def date_part(k):
+    sums = jnp.broadcast_to(jnp.sum(sums, 1, keepdims=True), sums.shape)
+    lane = lax.broadcasted_iota(jnp.int32, sums.shape, 1)
+    row = lax.broadcasted_iota(jnp.int32, sums.shape, 0)
+    part[...] = jnp.sum(jnp.where(lane == row, sums, 0.0), 0, keepdims=True)
+    here = s * pixes + q
+
+    def part_copy(k, kk):
         return pltpu.make_async_remote_copy(
-            part, part_date.at[s], pd_send.at[k], pd_recv.at[s],
-            device_id=(peer_of(k), q), device_id_type=MESH)
-
-    def pix_part(k):
-        return pltpu.make_async_remote_copy(
-            part_mid, part_pix.at[q], pp_send.at[k], pp_recv.at[q],
-            device_id=(s, lax.rem(q + k, pixes)), device_id_type=MESH)
-
-    for k in range(1, dates):
-        date_part(k).start()
-    part_date[s] = part[...]
-    for n in range(LAG):
-        relay(units * bands - LAG + n)
-    for k in range(1, dates):
-        sd = peer_of(k)
-        pltpu.make_async_copy(part_date.at[sd], part_date.at[sd], pd_recv.at[sd]).wait()
-    mid = part_date[0]
-    for sd in range(1, dates):
-        mid = mid + part_date[sd]
-    part_mid[...] = mid
-    for k in range(1, pixes):
-        pix_part(k).start()
-    part_pix[q] = mid
+            part, part_all.at[here], part_send.at[k, kk], part_recv.at[here],
+            device_id=(peer_of(k), lax.rem(q + kk, pixes)), device_id_type=MESH)
+
+    for k, kk in others:
+        part_copy(k, kk).start()
+    part_all[here] = part[...]
+    for n in range(LAG, DIRECT, -1):
+        relay(units * bands - n)
 
     @pl.loop(0, bands)
     def _(b):
         for r in range(per):
             pltpu.make_async_copy(fin.at[r, b], fin.at[r, b], fin_recv.at[r, b]).wait()
 
-    for k in range(1, pixes):
-        qq = lax.rem(q + k, pixes)
-        pltpu.make_async_copy(part_pix.at[qq], part_pix.at[qq], pp_recv.at[qq]).wait()
-    tot = part_pix[0]
-    for qq in range(1, pixes):
-        tot = tot + part_pix[qq]
-    tot_ref[...] = tot
+    for k, kk in others:
+        there = peer_of(k) * pixes + lax.rem(q + kk, pixes)
+        pltpu.make_async_copy(part_all.at[there], part_all.at[there], part_recv.at[there]).wait()
+    terms = [part_all[n] for n in range(dates * pixes)]
+    while len(terms) > 1:
+        terms = [sum(terms[i:i + 2]) for i in range(0, len(terms), 2)]
+    tot_ref[...] = terms[0]
 
     for k in range(1, dates):
         des_copy(k).wait_send()
-        date_part(k).wait_send()
-    for k in range(1, pixes):
-        pix_part(k).wait_send()
+    for k, kk in others:
+        part_copy(k, kk).wait_send()
 
     @pl.loop(0, units)
     def _(u):
@@ -381,8 +378,10 @@
 
     @pl.loop(0, bands)
     def _(b):
-        for r in range(per):
-            pass_on(r, b, False)
+        @pl.when((place // PAIR) * bands + b < units * bands - DIRECT)
+        def _():
+            for r in range(per):
+                pass_on(r, b, False)
 
 
 def put(res, u, b, i, value):
@@ -391,11 +390,12 @@
         res[u, b, jj, i] = whole[jj].astype(jnp.int16)
 
 
-def finish(fin, tot_ref, coef, score):
+def finish(fin, tot_ref, coef, score, coef_buf, score_buf, coef_sem, score_sem):
     per, bands = fin.shape[:2]
-    tot = jnp.sum(tot_ref[...], 1, keepdims=True)
+    copies = []
+    tot = tot_ref[...]
     for b in range(bands):
-        sigma = jnp.sqrt(tot[b:b + 1] / tot[bands:bands + 1])
+        sigma = jnp.sqrt(tot[:, b:b + 1] / tot[:, bands:bands + 1])
         scale = jnp.broadcast_to(1.0 / sigma, fin.shape[3:])
         for r in range(per):
             cols = slice(r * 128, (r + 1) * 128)
@@ -403,10 +403,16 @@
             unit = jnp.exp2(number(HARM + 1))
             step = unit * (1.0 / LIMIT)
             for i in range(HARM):
-                coef[b, i, :, cols] = number(i) * step
+                coef_buf[b, i, :, cols] = number(i) * step
             root = number(HARM) * (1.0 / LIMIT)
             root = root * root
-            score[b, :, cols] = root * root * (unit * scale)
+            score_buf[b, :, cols] = root * root * (unit * scale)
+        copies.append(pltpu.make_async_copy(coef_buf.at[b], coef.at[b], coef_sem.at[b]))
+        copies[-1].start()
+    copies.append(pltpu.make_async_copy(score_buf, score, score_sem))
+    copies[-1].start()
+    for c in copies:
+        c.wait()
 
 
 def local(mesh, stack, quality, days):
@@ -425,8 +431,8 @@
     fin, tot = pl.pallas_call(
         functools.partial(kernel, dims),
         out_shape=(
-            jax.ShapeDtypeStruct((per, bands, HARM + 2) + tile, jnp.int16),
-            jax.ShapeDtypeStruct((bands + 1, width), f32),
+            vmem((per, bands, HARM + 2) + tile, jnp.int16),
+            vmem((1, width), f32),
         ),
         in_specs=[
             pl.BlockSpec(memory_space=pl.ANY),
@@ -434,7 +440,7 @@
             pl.BlockSpec(memory_space=pltpu.SMEM),
         ],
         out_specs=(
-            pl.BlockSpec(memory_space=pl.ANY),
+            pl.BlockSpec(memory_space=pltpu.VMEM),
             pl.BlockSpec(memory_space=pltpu.VMEM),
         ),
         scratch_shapes=[
@@ -450,10 +456,8 @@
             vmem((units, bands, PAIR, HARM + 2) + tile, jnp.int16),
             vmem((per, bands, HARM + 2) + tile, jnp.int16),
             vmem((bands + 1,) + tile, f32),
-            vmem((bands + 1, width), f32),
-            vmem((dates, bands + 1, width), f32),
-            vmem((bands + 1, width), f32),
-            vmem((pixes, bands + 1, width), f32),
+            vmem((1, width), f32),
+            vmem((dates * pixes, 1, width), f32),
             dma,
             dma((dates,)),
             dma((dates,)),
@@ -463,24 +467,27 @@
             dma((per, bands)),
             dma((per, bands)),
             dma((per, bands)),
-            dma((dates,)),
-            dma((dates,)),
-            dma((pixes,)),
-            dma((pixes,)),
+            dma((dates, pixes)),
+            dma((dates * pixes,)),
         ],
         compiler_params=pltpu.CompilerParams(
             collective_id=0, has_side_effects=True, vmem_limit_bytes=60000000
         ),
     )(stack, quality, days)
     whole = pl.BlockSpec(memory_space=pltpu.VMEM)
+    there = pl.BlockSpec(memory_space=pl.ANY)
+    coef_shape = (bands, HARM, block, width * per)
+    score_shape = (bands, block, width * per)
     return pl.pallas_call(
         finish,
         out_shape=(
-            jax.ShapeDtypeStruct((bands, HARM, block, width * per), f32),
-            jax.ShapeDtypeStruct((bands, block, width * per), f32),
+            jax.ShapeDtypeStruct(coef_shape, f32),
+            jax.ShapeDtypeStruct(score_shape, f32),
         ),
         in_specs=[whole, whole],
-        out_specs=(whole, whole),
+        out_specs=(there, there),
+        scratch_shapes=[vmem(coef_shape, f32), vmem(score_shape, f32), dma((bands,)), dma],
+        compiler_params=pltpu.CompilerParams(vmem_limit_bytes=20000000),
     )(fin, tot)
 
 

time: 43.7 us -> 41.1 us (0.941)
  Pallas kernels: 42.9 us -> 40.3 us
    pallas_call x2, Pallas kernels: 42.9 us -> 40.3 us  [the longest x1 39.3 us: local(): pl.pallas_call(functools.partial(kernel, dims), out_shape=(vmem((per, ban...]
where the time goes in v2:
time: 41.1 us; the launch traced here: 40.9 us
  Pallas kernels  40.3 us (98%)
  between operations  0.64 us (2%)
    pallas_call x1, Pallas kernels, local(): pl.pallas_call(functools.partial(kernel, dims), out_shape=(vmem((per, ban...  39.3 us
    pallas_call x1, Pallas kernels, local(): pl.pallas_call(finish, out_shape=(jax.ShapeDtypeStruct(coef_shape, f32),...  0.94 us

profile of v2, /device:TPU:0, one launch (start us, length us, event | category | flops | bytes accessed | tf_op | source)
XLA Modules:
  0.0 40.9 jit_solution(7515573899152547182)
XLA Ops:
  0.6 39.3 %shard_map.50 = (s16[2,7,10,8,128]{4,3,2,1,0:T(8,128)(2,1)S(1)}, f32[1,128]{1,0:T(1,128)S(1)}) custom-call(bf16[16,7,64,128]{3,2,1,0:T(8,128)(2,1)} %stack.1, s32[16,64,128]{2,1,0:T(8,128)} %quality.1, s32[16]{0:T(128)} %days.1), custom_call_target="tpu_custom_call" | custom-call | tf_op jit(solution)/shard_map/pallas_call | solution.py:431
  40.0 0.9 %shard_map.51 = (f32[7,8,8,256]{3,2,1,0:T(8,128)}, f32[7,8,256]{2,1,0:T(8,128)}) custom-call(s16[2,7,10,8,128]{4,3,2,1,0:T(8,128)(2,1)S(1)} %get-tuple-element.4.fin, f32[1,128]{1,0:T(1,128)S(1)} %get-tuple-element.5.tot_ref), custom_call_target="tpu_custom_call" | custom-call | tf_op jit(solution)/shard_map/pallas_call | solution.py:481

commit v3 on v2

--- a/solution.py
+++ b/solution.py
@@ -12,6 +12,10 @@
 PAIR = 2
 LAG = 4
 DIRECT = 1
+MERGED = 6
+REST_AT = 5
+BEHIND = 4
+GRAM_AT = 2
 LIMIT = 32767.0
 LEVELS = 0x346C
 
@@ -33,10 +37,10 @@
 
 
 def kernel(dims, stack, quality, days, fin, tot_ref,
-           des_in, qbuf, code, raw, dall, bdes, wbuf, lbuf, wsum_ref, res, rel,
-           ssum, part, part_all,
-           q_sem, des_send, des_recv, raw_send, raw_recv,
-           hop_send, rel_recv, fin_send, fin_recv,
+           des_in, qbuf, code, raw, side, dall, bdes, wbuf, wside, gbuf, lbuf, lside,
+           wsum_ref, note_out, note_in, res, rel, ssum, part, part_all,
+           q_sem, des_send, des_recv, raw_send, raw_recv, side_send, side_recv,
+           next_send, note_send, note_recv, hop_send, rel_recv, fin_send, fin_recv,
            part_send, part_recv):
     dates, pixes, times, bands, block = dims
     per = pixes // dates
@@ -47,6 +51,9 @@
     total = dates * times
     place = lax.rem(q, per)
     home = q // per
+    merged = merged_bands(dates, bands)
+    along = 1 + lax.rem(q, 2)
+    across = 3 - along
 
     def peer_of(k):
         if dates & (dates - 1):
@@ -88,6 +95,10 @@
             pltpu.make_async_copy(
                 stack.at[:, b, rows_of(mine, u), :], raw.at[u, b, mine_at(s)],
                 raw_recv.at[u, b, s]).start()
+            if b < merged:
+                pltpu.make_async_copy(
+                    stack.at[:, b, rows_of(group(peer_of(along)), u), :],
+                    side.at[u, b, pl.ds(0, times)], side_recv.at[u, b, 0]).start()
 
     des_in[...] = design_lanes([days[r] for r in range(times)])
     q_copy.wait()
@@ -107,33 +118,70 @@
             des_in, dall.at[s], des_send.at[k], des_recv.at[s],
             device_id=(peer_of(k), q), device_id_type=MESH)
 
-    def raw_copy(u, b, k):
-        peer = peer_of(k)
+    def values_of(u, b, k):
+        return stack.at[:, b, rows_of(group(peer_of(k)), u), :]
+
+    def codes_of(u, k):
+        return code.at[group(peer_of(k)), u]
+
+    def raw_copy(src, u, b, k, slot):
         return pltpu.make_async_remote_copy(
-            stack.at[:, b, rows_of(group(peer), u), :], raw.at[u, b, mine_at(s)],
-            raw_send.at[u, b, k], raw_recv.at[u, b, s],
-            device_id=(peer, q), device_id_type=MESH)
-
-    def code_copy(u, k):
-        peer = peer_of(k)
+            src, raw.at[u, b, mine_at(s)], raw_send.at[u, b, slot], raw_recv.at[u, b, s],
+            device_id=(peer_of(k), q), device_id_type=MESH)
+
+    def side_copy(src, u, b):
         return pltpu.make_async_remote_copy(
-            code.at[group(peer), u], raw.at[u, bands, mine_at(s)],
-            raw_send.at[u, bands, k], raw_recv.at[u, bands, s],
-            device_id=(peer, q), device_id_type=MESH)
-
-    order = range(dates - 1, 0, -1)
+            src, side.at[u, b, pl.ds(times, times)], side_send.at[u, b], side_recv.at[u, b, 1],
+            device_id=(peer_of(across), q), device_id_type=MESH)
+
+    def next_copy(u):
+        first = peer_of(across)
+        return pltpu.make_async_remote_copy(
+            side.at[u, merged, pl.ds(times, times)], raw.at[u, bands, mine_at(first)],
+            next_send.at[u], raw_recv.at[u, bands, first],
+            device_id=(peer_of(along), q), device_id_type=MESH)
+
+    def note_copy(u, b):
+        return pltpu.make_async_remote_copy(
+            note_out.at[u, b], note_in.at[u, b], note_send.at[u, b], note_recv.at[u, b],
+            device_id=(peer_of(along), q), device_id_type=MESH)
+
+    order = list(range(dates - 1, 0, -1))
+
+    def code_copies(u):
+        if not merged:
+            return [raw_copy(codes_of(u, k), u, bands, k, k) for k in order]
+        return [side_copy(codes_of(u, dates - 1), u, merged),
+                raw_copy(codes_of(u, across), u, bands, across, 1),
+                raw_copy(codes_of(u, along), u, bands, along, 2)]
+
+    def merged_copies(u, b):
+        return [side_copy(values_of(u, b, dates - 1), u, b),
+                raw_copy(values_of(u, b, across), u, b, across, 1)]
+
+    def rest_copies(u, b):
+        return [raw_copy(values_of(u, b, k), u, b, k, k) for k in order]
+
     for k in order:
         des_copy(k).start()
     for u in range(units):
-        for k in order:
-            code_copy(u, k).start()
-        for b in range(bands):
-            for k in order:
-                raw_copy(u, b, k).start()
+        for c in code_copies(u):
+            c.start()
+        for b in range(merged):
+            for c in merged_copies(u, b):
+                c.start()
+        if not merged:
+            for b in range(bands):
+                for c in rest_copies(u, b):
+                    c.start()
     for u in range(units):
         pltpu.make_async_copy(
             code.at[mine, u], raw.at[u, bands, mine_at(s)],
             raw_recv.at[u, bands, s]).start()
+        if merged:
+            pltpu.make_async_copy(
+                code.at[group(peer_of(along)), u], side.at[u, merged, pl.ds(0, times)],
+                side_recv.at[u, merged, 0]).start()
 
     def raw_wait(u, b, sd):
         there = raw.at[u, b, mine_at(sd)]
@@ -146,42 +194,49 @@
     for b in range(bands + 1):
         ssum[b] = zero_one
 
-    def spread(k):
+    def side_wait(u, b, slot):
+        there = side.at[u, b, pl.ds(pl.multiple_of(slot * times, times), times)]
+        pltpu.make_async_copy(there, there, side_recv.at[u, b, slot]).wait()
+
+    def spread(k, wait):
         sd = peer_of(k)
-        if k:
+        if wait:
             pltpu.make_async_copy(dall.at[sd], dall.at[sd], des_recv.at[sd]).wait()
 
-        @pl.loop(0, times, unroll=4)
-        def _(r):
-            row = dall[sd, pl.ds(r, 1), :]
-            for i in range(HARM):
-                bdes[sd * times + r, i] = jnp.broadcast_to(row[:, i:i + 1], (block, 128))
-
-    for k in range(dates):
-        spread(k)
+        rows = dall[sd]
+        for i in range(HARM):
+            bdes[i, mine_at(sd), :] = jnp.broadcast_to(rows[:, i:i + 1], rows.shape)
+
+    def design(t, i):
+        return jnp.broadcast_to(bdes[i, pl.ds(t, 1), :], (block, 128))
 
     def pair_of(value):
         return value.astype(jnp.float32).reshape(PAIR, block, 128)
 
-    def by_source(wait, body, carry, unroll):
-        def source(k, carry):
-            sd = peer_of(k)
-            wait(sd)
+    def by_source(count, source_of, wait, body, carry, unroll):
+        def source(n, carry):
+            sd = source_of(n)
+            wait(n, sd)
             return lax.fori_loop(
-                0, times, lambda r, c: body(sd * times + r, c), carry, unroll=unroll)
-
-        return lax.fori_loop(0, dates, source, carry)
-
-    def gram_step(u):
+                0, times, lambda r, c: body(sd * times + r, n * times + r, c), carry,
+                unroll=unroll)
+
+        return lax.fori_loop(0, count, source, carry)
+
+    every = (dates, peer_of)
+    near = (2, lambda n: peer_of(n * across)) if merged else every
+    far = (2, lambda n: peer_of(along + n * (dates - 1 - along)))
+
+    def gram_over(sources, wait, code_at, weight_at, weight_to, out):
         def body(jj):
-            def step(t, carry):
+            def step(t, place_t, carry):
                 if jj == 0:
-                    both = pair_of(raw[u, bands, t]) * (1.0 / 12.0)
-                    wbuf[t] = both
+                    both = pair_of(code_at(t, place_t)) * (1.0 / 12.0)
+                    weight_to(t, place_t, both)
                     w = both[0]
                 else:
-                    w = wbuf[t, jj]
-                d = [bdes[t, i] for i in range(HARM)]
+                    w = weight_at(t, place_t, jj)
+                d = [design(t, i) for i in range(HARM)]
                 wd = [w] + [w * d[i] for i in range(1, HARM)]
                 return tuple(
                     carry[n] + (wd[first] if second == 0 else wd[first] * d[second])
@@ -189,16 +244,13 @@
             return step
 
         start = (zero_one,) * len(PAIR_LIST)
-        gram = by_source(lambda sd: raw_wait(u, bands, sd), body(0), start, 2)
-        for n in range(len(PAIR_LIST)):
-            lbuf[n, 0] = gram[n]
-        for jj in range(1, PAIR):
-            gram = lax.fori_loop(0, total, body(jj), start, unroll=2)
+        for jj in range(PAIR):
+            gram = by_source(
+                *sources, wait if jj == 0 else lambda n, sd: None, body(jj), start, 2)
             for n in range(len(PAIR_LIST)):
-                lbuf[n, jj] = gram[n]
-        gram = [lbuf[n] for n in range(len(PAIR_LIST))]
-        wsum_ref[...] = 1.0 / (gram[0] + 1.0)
-        ssum[bands] = ssum[bands] + jnp.sum(gram[0], 0)
+                out[n, jj] = gram[n]
+
+    def factor(gram, out):
         lower = {}
         for first in range(HARM):
             for second in range(first + 1):
@@ -211,50 +263,10 @@
                     lower[first, first] = lax.rsqrt(value)
                 else:
                     lower[first, second] = value * lower[second, second]
-                lbuf[PAIR_AT[first, second]] = lower[first, second]
-
-    def hop(u, b, start):
-        for jj in range(PAIR):
-            p = mine * per + PAIR * u + jj
-
-            def act(dst, sem):
-                @pl.when(p != q)
-                def _():
-                    c = pltpu.make_async_remote_copy(
-                        res.at[u, b, jj], dst, hop_send.at[u, b, jj], sem,
-                        device_id=(s, p), device_id_type=MESH)
-                    c.start() if start else c.wait_send()
-
-                if start:
-                    @pl.when(p == q)
-                    def _():
-                        pltpu.make_async_copy(res.at[u, b, jj], dst, sem).start()
-
-            @pl.when(home == s)
-            def _():
-                act(fin.at[place, b], fin_recv.at[place, b])
-
-            late = u * bands + b >= units * bands - DIRECT
-
-            @pl.when(jnp.logical_and(home != s, jnp.logical_not(late)))
-            def _():
-                act(rel.at[place, b], rel_recv.at[place, b])
-
-            @pl.when(jnp.logical_and(home != s, late))
-            def _():
-                c = pltpu.make_async_remote_copy(
-                    res.at[u, b, jj], fin.at[place, b], hop_send.at[u, b, jj],
-                    fin_recv.at[place, b], device_id=(home, p), device_id_type=MESH)
-                c.start() if start else c.wait_send()
-
-    def band_step(u, b):
-        def body(t, carry):
-            wy = wbuf[t] * pair_of(raw[u, b, t])
-            return tuple(
-                carry[i] + (wy if i == 0 else bdes[t, i] * wy) for i in range(HARM))
-
-        moment = by_source(lambda sd: raw_wait(u, b, sd), body, (zero,) * HARM, 8)
-        low = lambda first, second: lbuf[PAIR_AT[first, second]]
+                out[PAIR_AT[first, second]] = lower[first, second]
+
+    def solve(moment, lref):
+        low = lambda first, second: lref[PAIR_AT[first, second]]
         forward = []
         for first in range(HARM):
             value = moment[first]
@@ -267,15 +279,136 @@
             for inner in range(HARM - 1, first, -1):
                 value = value - low(inner, first) * back[inner]
             back[first] = value * low(first, first)
-
-        def residual(t, ssr):
-            terms = [back[0]] + [bdes[t, i] * back[i] for i in range(1, HARM)]
+        return back
+
+    def moment_over(sources, wait, value_at, weight_at):
+        def body(t, place_t, carry):
+            wy = weight_at(t, place_t) * pair_of(value_at(t, place_t))
+            return tuple(
+                carry[i] + (wy if i == 0 else design(t, i) * wy) for i in range(HARM))
+
+        return by_source(*sources, wait, body, (zero,) * HARM, 8)
+
+    def residual_over(sources, back, value_at, weight_at):
+        def body(t, place_t, ssr):
+            terms = [back[0]] + [design(t, i) * back[i] for i in range(1, HARM)]
             while len(terms) > 1:
                 terms = [terms[i] + terms[i + 1] for i in range(0, len(terms), 2)]
-            diff = pair_of(raw[u, b, t]) - terms[0]
-            return ssr + wbuf[t] * diff * diff
-
-        ssr = lax.fori_loop(0, total, residual, zero, unroll=8)
+            diff = pair_of(value_at(t, place_t)) - terms[0]
+            return ssr + weight_at(t, place_t) * diff * diff
+
+        return by_source(*sources, lambda n, sd: None, body, zero, 8)
+
+    def side_gram(u):
+        def wait(n, sd):
+            side_wait(u, merged, n)
+
+            @pl.when(n == 1)
+            def _():
+                next_copy(u).start()
+
+        def keep(t, place_t, both):
+            wside[place_t] = both
+
+        gram_over(near, wait, lambda t, place_t: side[u, merged, place_t],
+                  lambda t, place_t, jj: wside[place_t, jj], keep, lside)
+        factor([lside[n] for n in range(len(PAIR_LIST))], lside)
+
+    def side_step(u, b):
+        value_at = lambda t, place_t: side[u, b, place_t]
+        weight_at = lambda t, place_t: wside[place_t]
+        moment = moment_over(near, lambda n, sd: side_wait(u, b, n), value_at, weight_at)
+        back = solve(moment, lside)
+        for i in range(HARM):
+            note_out[u, b, i] = back[i]
+        note_out[u, b, HARM] = residual_over(near, back, value_at, weight_at)
+        note_copy(u, b).start()
+
+    def own_gram(u):
+        def keep(t, place_t, both):
+            wbuf[t] = both
+
+        def over(sources, out):
+            gram_over(sources, lambda n, sd: raw_wait(u, bands, sd),
+                      lambda t, place_t: raw[u, bands, t],
+                      lambda t, place_t, jj: wbuf[t, jj], keep, out)
+
+        over(near, lbuf)
+        if merged:
+            over(far, gbuf)
+            gram = [lbuf[n] + gbuf[n] for n in range(len(PAIR_LIST))]
+        else:
+            gram = [lbuf[n] for n in range(len(PAIR_LIST))]
+        wsum_ref[...] = 1.0 / (gram[0] + 1.0)
+        ssum[bands] = ssum[bands] + jnp.sum(gram[0], 0)
+        factor(gram, lbuf)
+
+    def far_gram_times(vector):
+        rows = []
+        for first in range(HARM):
+            row = None
+            for second in range(HARM):
+                pair = (max(first, second), min(first, second))
+                term = gbuf[PAIR_AT[pair]] * vector[second]
+                row = term if row is None else row + term
+            rows.append(row)
+        return rows
+
+    def hop(u, b, start):
+        for jj in range(PAIR):
+            p = mine * per + PAIR * u + jj
+
+            def act(dst, sem):
+                @pl.when(p != q)
+                def _():
+                    c = pltpu.make_async_remote_copy(
+                        res.at[u, b, jj], dst, hop_send.at[u, b, jj], sem,
+                        device_id=(s, p), device_id_type=MESH)
+                    c.start() if start else c.wait_send()
+
+                if start:
+                    @pl.when(p == q)
+                    def _():
+                        pltpu.make_async_copy(res.at[u, b, jj], dst, sem).start()
+
+            @pl.when(home == s)
+            def _():
+                act(fin.at[place, b], fin_recv.at[place, b])
+
+            late = u * bands + b >= units * bands - DIRECT
+
+            @pl.when(jnp.logical_and(home != s, jnp.logical_not(late)))
+            def _():
+                act(rel.at[place, b], rel_recv.at[place, b])
+
+            @pl.when(jnp.logical_and(home != s, late))
+            def _():
+                c = pltpu.make_async_remote_copy(
+                    res.at[u, b, jj], fin.at[place, b], hop_send.at[u, b, jj],
+                    fin_recv.at[place, b], device_id=(home, p), device_id_type=MESH)
+                c.start() if start else c.wait_send()
+
+    def band_step(u, b, with_note):
+        value_at = lambda t, place_t: raw[u, b, t]
+        weight_at = lambda t, place_t: wbuf[t]
+        sources = near if with_note else every
+        moment = moment_over(
+            sources, lambda n, sd: raw_wait(u, b, sd), value_at, weight_at)
+        if with_note:
+            pltpu.make_async_copy(note_in.at[u, b], note_in.at[u, b], note_recv.at[u, b]).wait()
+            fit = [note_in[u, b, i] for i in range(HARM)]
+            rows = far_gram_times(fit)
+            moment = [moment[i] + (rows[i] + fit[i]) for i in range(HARM)]
+        back = solve(moment, lbuf)
+        ssr = residual_over(sources, back, value_at, weight_at)
+        if with_note:
+            fit = [note_in[u, b, i] for i in range(HARM)]
+            shift = [back[i] - fit[i] for i in range(HARM)]
+            rows = far_gram_times(shift)
+            extra = note_in[u, b, HARM]
+            for i in range(HARM):
+                extra = extra + shift[i] * (rows[i] - 2.0 * fit[i])
+            ssr = jnp.maximum(ssr + extra, 0.0)
         ratio = jnp.sqrt(ssr * wsum_ref[...])
         peak = ratio
         for i in range(HARM):
@@ -313,20 +446,64 @@
             for r in range(per):
                 pass_on(r, b, True)
 
-    @pl.loop(0, units * bands)
+    def rest_at(u, act):
+        for b in range(merged, bands):
+            for c in rest_copies(u, b):
+                act(c)
+
+    if merged:
+        spread(0, False)
+        spread(across, True)
+    else:
+        for k in range(dates):
+            spread(k, k > 0)
+
+    behind = BEHIND if merged else 1
+    gram_at = GRAM_AT if merged else 0
+    steps = bands + behind
+
+    @pl.loop(0, units * steps)
     def _(n):
-        u = n // bands
-        b = lax.rem(n, bands)
-
-        @pl.when(b == 0)
+        u = n // steps
+        step = lax.rem(n, steps)
+        if merged:
+            @pl.when(step == 0)
+            def _():
+                side_gram(u)
+
+            @pl.when(step < merged)
+            def _():
+                side_step(u, step)
+
+            @pl.when(n == 0)
+            def _():
+                spread(along, True)
+                spread(dates - 1, True)
+
+            @pl.when(step == REST_AT)
+            def _():
+                rest_at(u, lambda c: c.start())
+
+        @pl.when(step == gram_at)
         def _():
-            gram_step(u)
-
-        band_step(u, b)
-
-        @pl.when(n >= LAG)
+            own_gram(u)
+
+        b = step - behind
+        if merged:
+            @pl.when(jnp.logical_and(b >= 0, b < merged))
+            def _():
+                band_step(u, b, True)
+
+        if merged < bands:
+            @pl.when(b >= merged)
+            def _():
+                band_step(u, b, False)
+
+        done = u * bands + b
+
+        @pl.when(jnp.logical_and(b >= 0, done >= LAG))
         def _():
-            relay(n - LAG)
+            relay(done - LAG)
 
     sums = jnp.concatenate(
         [jnp.sum(ssum[b], 0, keepdims=True) for b in range(bands + 1)], 0)
@@ -367,13 +544,25 @@
 
     @pl.loop(0, units)
     def _(u):
-        for k in range(1, dates):
-            code_copy(u, k).wait_send()
+        for c in code_copies(u):
+            c.wait_send()
+        if merged:
+            next_copy(u).wait_send()
+
+            @pl.loop(0, merged)
+            def _(b):
+                for c in merged_copies(u, b):
+                    c.wait_send()
+                note_copy(u, b).wait_send()
+            rest_at(u, lambda c: c.wait_send())
+        else:
+            @pl.loop(0, bands)
+            def _(b):
+                for c in rest_copies(u, b):
+                    c.wait_send()
 
         @pl.loop(0, bands)
         def _(b):
-            for k in range(1, dates):
-                raw_copy(u, b, k).wait_send()
             hop(u, b, False)
 
     @pl.loop(0, bands)
@@ -382,6 +571,10 @@
         def _():
             for r in range(per):
                 pass_on(r, b, False)
+
+
+def merged_bands(dates, bands):
+    return min(MERGED, bands - 1) if dates == 4 else 0
 
 
 def put(res, u, b, i, value):
@@ -423,6 +616,8 @@
     units = per // PAIR
     total = dates * times
     dims = (dates, pixes, times, bands, block)
+    merged = merged_bands(dates, bands)
+    notes = max(merged, 1)
     tile = (block, width)
     both = (PAIR,) + tile
     tall = (PAIR * block, width)
@@ -448,11 +643,17 @@
             vmem((times, rows, width), jnp.int32),
             vmem((dates, units, times) + tall, bf16),
             vmem((units, bands + 1, total) + tall, bf16),
+            vmem((units, merged + 1, 2 * times) + tall, bf16),
             vmem((dates, times, 128), f32),
-            vmem((total, HARM) + tile, f32),
+            vmem((HARM, total, width), f32),
             vmem((total,) + both, f32),
+            vmem((2 * times,) + both, f32),
+            vmem((len(PAIR_LIST),) + both, f32),
+            vmem((len(PAIR_LIST),) + both, f32),
             vmem((len(PAIR_LIST),) + both, f32),
             vmem(both, f32),
+            vmem((units, notes, HARM + 1) + both, f32),
+            vmem((units, notes, HARM + 1) + both, f32),
             vmem((units, bands, PAIR, HARM + 2) + tile, jnp.int16),
             vmem((per, bands, HARM + 2) + tile, jnp.int16),
             vmem((bands + 1,) + tile, f32),
@@ -463,6 +664,11 @@
             dma((dates,)),
             dma((units, bands + 1, dates)),
             dma((units, bands + 1, dates)),
+            dma((units, merged + 1)),
+            dma((units, merged + 1, 2)),
+            dma((units,)),
+            dma((units, notes)),
+            dma((units, notes)),
             dma((units, bands, PAIR)),
             dma((per, bands)),
             dma((per, bands)),

time: 41.1 us -> 38.5 us (0.937)
  Pallas kernels: 40.3 us -> 37.7 us
    pallas_call x1, Pallas kernels: 39.3 us -> 36.8 us  [local(): pl.pallas_call(functools.partial(kernel, dims), out_shape=(vmem((per, ban...]
where the time goes in v3:
time: 38.5 us; the launch traced here: 38.4 us
  Pallas kernels  37.7 us (98%)
  between operations  0.64 us (2%)
    pallas_call x1, Pallas kernels, local(): pl.pallas_call(functools.partial(kernel, dims), out_shape=(vmem((per, ban...  36.8 us
    pallas_call x1, Pallas kernels, local(): pl.pallas_call(finish, out_shape=(jax.ShapeDtypeStruct(coef_shape, f32),...  0.94 us

profile of v3, /device:TPU:0, one launch (start us, length us, event | category | flops | bytes accessed | tf_op | source)
XLA Modules:
  0.0 38.4 jit_solution(2201884392849245952)
XLA Ops:
  0.6 36.8 %shard_map.50 = (s16[2,7,10,8,128]{4,3,2,1,0:T(8,128)(2,1)S(1)}, f32[1,128]{1,0:T(1,128)S(1)}) custom-call(bf16[16,7,64,128]{3,2,1,0:T(8,128)(2,1)} %stack.1, s32[16,64,128]{2,1,0:T(8,128)} %quality.1, s32[16]{0:T(128)} %days.1), custom_call_target="tpu_custom_call" | custom-call | tf_op jit(solution)/shard_map/pallas_call | solution.py:626
  37.4 0.9 %shard_map.51 = (f32[7,8,8,256]{3,2,1,0:T(8,128)}, f32[7,8,256]{2,1,0:T(8,128)}) custom-call(s16[2,7,10,8,128]{4,3,2,1,0:T(8,128)(2,1)S(1)} %get-tuple-element.4.fin, f32[1,128]{1,0:T(1,128)S(1)} %get-tuple-element.5.tot_ref), custom_call_target="tpu_custom_call" | custom-call | tf_op jit(solution)/shard_map/pallas_call | solution.py:687

commit v4 on v3

--- a/solution.py
+++ b/solution.py
@@ -14,6 +14,7 @@
 DIRECT = 1
 MERGED = 6
 REST_AT = 5
+AHEAD = 1
 BEHIND = 4
 GRAM_AT = 2
 LIMIT = 32767.0
@@ -156,8 +157,8 @@
                 raw_copy(codes_of(u, along), u, bands, along, 2)]
 
     def merged_copies(u, b):
-        return [side_copy(values_of(u, b, dates - 1), u, b),
-                raw_copy(values_of(u, b, across), u, b, across, 1)]
+        return [lambda: side_copy(values_of(u, b, dates - 1), u, b),
+                lambda: raw_copy(values_of(u, b, across), u, b, across, 1)]
 
     def rest_copies(u, b):
         return [raw_copy(values_of(u, b, k), u, b, k, k) for k in order]
@@ -167,9 +168,11 @@
     for u in range(units):
         for c in code_copies(u):
             c.start()
-        for b in range(merged):
-            for c in merged_copies(u, b):
-                c.start()
+        for b in range(merged + AHEAD):
+            if b < merged:
+                merged_copies(u, b)[0]().start()
+            if b >= AHEAD:
+                merged_copies(u, b - AHEAD)[1]().start()
         if not merged:
             for b in range(bands):
                 for c in rest_copies(u, b):
@@ -552,7 +555,7 @@
             @pl.loop(0, merged)
             def _(b):
                 for c in merged_copies(u, b):
-                    c.wait_send()
+                    c().wait_send()
                 note_copy(u, b).wait_send()
             rest_at(u, lambda c: c.wait_send())
         else:

time: 38.5 us -> 37.8 us (0.982)
  Pallas kernels: 37.7 us -> 37 us
    pallas_call x1, Pallas kernels: 36.8 us -> 36.1 us  [local(): pl.pallas_call(functools.partial(kernel, dims), out_shape=(vmem((per, ban...]
where the time goes in v4:
time: 37.8 us; the launch traced here: 37.7 us
  Pallas kernels  37 us (98%)
  between operations  0.64 us (2%)
    pallas_call x1, Pallas kernels, local(): pl.pallas_call(functools.partial(kernel, dims), out_shape=(vmem((per, ban...  36.1 us
    pallas_call x1, Pallas kernels, local(): pl.pallas_call(finish, out_shape=(jax.ShapeDtypeStruct(coef_shape, f32),...  0.94 us

profile of v4, /device:TPU:0, one launch (start us, length us, event | category | flops | bytes accessed | tf_op | source)
XLA Modules:
  0.0 37.7 jit_solution(1125448513169362565)
XLA Ops:
  0.6 36.1 %shard_map.50 = (s16[2,7,10,8,128]{4,3,2,1,0:T(8,128)(2,1)S(1)}, f32[1,128]{1,0:T(1,128)S(1)}) custom-call(bf16[16,7,64,128]{3,2,1,0:T(8,128)(2,1)} %stack.1, s32[16,64,128]{2,1,0:T(8,128)} %quality.1, s32[16]{0:T(128)} %days.1), custom_call_target="tpu_custom_call" | custom-call | tf_op jit(solution)/shard_map/pallas_call | solution.py:629
  36.7 0.9 %shard_map.51 = (f32[7,8,8,256]{3,2,1,0:T(8,128)}, f32[7,8,256]{2,1,0:T(8,128)}) custom-call(s16[2,7,10,8,128]{4,3,2,1,0:T(8,128)(2,1)S(1)} %get-tuple-element.4.fin, f32[1,128]{1,0:T(1,128)S(1)} %get-tuple-element.5.tot_ref), custom_call_target="tpu_custom_call" | custom-call | tf_op jit(solution)/shard_map/pallas_call | solution.py:690

commit v5 on v4

--- a/solution.py
+++ b/solution.py
@@ -521,24 +521,11 @@
             part, part_all.at[here], part_send.at[k, kk], part_recv.at[here],
             device_id=(peer_of(k), lax.rem(q + kk, pixes)), device_id_type=MESH)
 
-    for k, kk in others:
+    for k, kk in reversed(others):
         part_copy(k, kk).start()
     part_all[here] = part[...]
     for n in range(LAG, DIRECT, -1):
         relay(units * bands - n)
-
-    @pl.loop(0, bands)
-    def _(b):
-        for r in range(per):
-            pltpu.make_async_copy(fin.at[r, b], fin.at[r, b], fin_recv.at[r, b]).wait()
-
-    for k, kk in others:
-        there = peer_of(k) * pixes + lax.rem(q + kk, pixes)
-        pltpu.make_async_copy(part_all.at[there], part_all.at[there], part_recv.at[there]).wait()
-    terms = [part_all[n] for n in range(dates * pixes)]
-    while len(terms) > 1:
-        terms = [sum(terms[i:i + 2]) for i in range(0, len(terms), 2)]
-    tot_ref[...] = terms[0]
 
     for k in range(1, dates):
         des_copy(k).wait_send()
@@ -574,6 +561,19 @@
         def _():
             for r in range(per):
                 pass_on(r, b, False)
+
+    @pl.loop(0, bands)
+    def _(b):
+        for r in range(per):
+            pltpu.make_async_copy(fin.at[r, b], fin.at[r, b], fin_recv.at[r, b]).wait()
+
+    for k, kk in others:
+        there = peer_of(k) * pixes + lax.rem(q + kk, pixes)
+        pltpu.make_async_copy(part_all.at[there], part_all.at[there], part_recv.at[there]).wait()
+    terms = [part_all[n] for n in range(dates * pixes)]
+    while len(terms) > 1:
+        terms = [sum(terms[i:i + 2]) for i in range(0, len(terms), 2)]
+    tot_ref[...] = terms[0]
 
 
 def merged_bands(dates, bands):

time: 37.8 us -> 37.5 us (level)
  no operation moved by 1% of the time
where the time goes in v5:
time: 37.5 us; the launch traced here: 37.4 us
  Pallas kernels  36.7 us (98%)
  between operations  0.64 us (2%)
    pallas_call x1, Pallas kernels, local(): pl.pallas_call(functools.partial(kernel, dims), out_shape=(vmem((per, ban...  35.8 us
    pallas_call x1, Pallas kernels, local(): pl.pallas_call(finish, out_shape=(jax.ShapeDtypeStruct(coef_shape, f32),...  0.94 us

profile of v5, /device:TPU:0, one launch (start us, length us, event | category | flops | bytes accessed | tf_op | source)
XLA Modules:
  0.0 37.4 jit_solution(13020097292731520089)
XLA Ops:
  0.6 35.8 %shard_map.50 = (s16[2,7,10,8,128]{4,3,2,1,0:T(8,128)(2,1)S(1)}, f32[1,128]{1,0:T(1,128)S(1)}) custom-call(bf16[16,7,64,128]{3,2,1,0:T(8,128)(2,1)} %stack.1, s32[16,64,128]{2,1,0:T(8,128)} %quality.1, s32[16]{0:T(128)} %days.1), custom_call_target="tpu_custom_call" | custom-call | tf_op jit(solution)/shard_map/pallas_call | solution.py:629
  36.4 0.9 %shard_map.51 = (f32[7,8,8,256]{3,2,1,0:T(8,128)}, f32[7,8,256]{2,1,0:T(8,128)}) custom-call(s16[2,7,10,8,128]{4,3,2,1,0:T(8,128)(2,1)S(1)} %get-tuple-element.4.fin, f32[1,128]{1,0:T(1,128)S(1)} %get-tuple-element.5.tot_ref), custom_call_target="tpu_custom_call" | custom-call | tf_op jit(solution)/shard_map/pallas_call | solution.py:690

commit v6 on v5

--- a/solution.py
+++ b/solution.py
@@ -11,7 +11,7 @@
 HARM = 8
 PAIR = 2
 LAG = 4
-DIRECT = 1
+DIRECT = 2
 MERGED = 6
 REST_AT = 5
 AHEAD = 1

time: 37.5 us -> 37.5 us (level)
  no operation moved by 1% of the time
where the time goes in v6:
time: 37.5 us; the launch traced here: 37.3 us
  Pallas kernels  36.7 us (98%)
  between operations  0.64 us (2%)
    pallas_call x1, Pallas kernels, local(): pl.pallas_call(functools.partial(kernel, dims), out_shape=(vmem((per, ban...  35.7 us
    pallas_call x1, Pallas kernels, local(): pl.pallas_call(finish, out_shape=(jax.ShapeDtypeStruct(coef_shape, f32),...  0.94 us

profile of v6, /device:TPU:0, one launch (start us, length us, event | category | flops | bytes accessed | tf_op | source)
XLA Modules:
  0.0 37.3 jit_solution(12999183763238182904)
XLA Ops:
  0.6 35.7 %shard_map.50 = (s16[2,7,10,8,128]{4,3,2,1,0:T(8,128)(2,1)S(1)}, f32[1,128]{1,0:T(1,128)S(1)}) custom-call(bf16[16,7,64,128]{3,2,1,0:T(8,128)(2,1)} %stack.1, s32[16,64,128]{2,1,0:T(8,128)} %quality.1, s32[16]{0:T(128)} %days.1), custom_call_target="tpu_custom_call" | custom-call | tf_op jit(solution)/shard_map/pallas_call | solution.py:629
  36.4 0.9 %shard_map.51 = (f32[7,8,8,256]{3,2,1,0:T(8,128)}, f32[7,8,256]{2,1,0:T(8,128)}) custom-call(s16[2,7,10,8,128]{4,3,2,1,0:T(8,128)(2,1)S(1)} %get-tuple-element.4.fin, f32[1,128]{1,0:T(1,128)S(1)} %get-tuple-element.5.tot_ref), custom_call_target="tpu_custom_call" | custom-call | tf_op jit(solution)/shard_map/pallas_call | solution.py:690
